TPU v7x, 128 devices: a whole 4x4x4 slice. The times are simulated.
128 devices in a mesh: seq: 16 (over x_hi, z, core), tp: 8 (over y, x_lo).
Axes of the slice: x: 4 (x_hi: 2, x_lo: 2; x = x_hi * 2 + x_lo), y: 4, z: 4, core: 2. Of those that a mesh axis runs over, the one named last changes fastest.
Arguments:
- tokens: bfloat16 [2048, 8192], P('seq'), may hold values from -6 to 6
- conv_weight: float32 [4, 8192], replicated, may hold values from -3 to 3
- norm_gain: float32 [8192], replicated, may hold values from 0.25 to 1.75
- gate_weight: bfloat16 [8192, 14336], P('seq', 'tp'), may hold values from -0.0625 to 0.0625
- up_weight: bfloat16 [8192, 14336], P('seq', 'tp'), may hold values from -0.0625 to 0.0625
- down_weight: bfloat16 [14336, 8192], P('tp', 'seq'), may hold values from -0.046875 to 0.046875
Outputs:
- mixed_out: bfloat16 [2048, 8192], P(('seq', 'tp'))
All inputs are finite; a program needn't handle non-finite values.
Results may differ from a plain program's by a relative error of at most 0.03.
Values may be sent and summed in bfloat16 or wider, within the bound.
No kernel may reach another device: no remote copies, remote signals or barrier semaphores. Data moves between devices by JAX's collectives and lax.ppermute only.
A program may use at most 64 MiB of HBM per device.

v0:
```python
import jax
import jax.numpy as jnp
from jax import lax
from jax.sharding import PartitionSpec as P


def from_behind(shard, axis, by):
    peers = lax.axis_size(axis)
    pairs = [(i, i + by) for i in range(peers) if 0 <= i + by < peers]
    return lax.ppermute(shard, axis, pairs)


def split_up(shard, dim, peers):
    shape = shard.shape
    parts = shard.reshape(*shape[:dim], peers, shape[dim] // peers, *shape[dim + 1 :])
    return jnp.moveaxis(parts, dim, 0)


def summed_on_arrival(shard, axis, dim):
    parts = split_up(shard, dim, lax.axis_size(axis))
    arrived = lax.all_to_all(parts, axis, split_axis=0, concat_axis=0, tiled=True)
    return arrived.astype(jnp.float32).sum(axis=0)


def swiglu(both_sums, half_cols):
    return (jax.nn.silu(both_sums[:, :half_cols]) * both_sums[:, half_cols:]).astype(jnp.bfloat16)


def shards(tokens, conv_weight, norm_gain, gate_weight, up_weight, down_weight):
    tok_rows = tokens.shape[0]
    taps_count = conv_weight.shape[0]
    seq_count = lax.axis_size("seq")
    edge_rows = from_behind(tokens[tok_rows - (taps_count - 1) :], "seq", 1)
    extended = jnp.concatenate([edge_rows, tokens], 0).astype(jnp.float32)
    conv_out = jnp.zeros(tokens.shape, jnp.float32)
    for tap_index in range(taps_count):
        begin = taps_count - 1 - tap_index
        conv_out = conv_out + conv_weight[tap_index][None, :] * extended[begin : begin + tok_rows]
    scale_rms = lax.rsqrt(jnp.mean(conv_out * conv_out, axis=-1, keepdims=True) + 1e-05)
    normed = (conv_out * scale_rms * norm_gain[None, :]).astype(jnp.bfloat16)
    all_rows = lax.all_to_all(normed, "seq", split_axis=1, concat_axis=0, tiled=True)
    half_cols = gate_weight.shape[1]
    w_both = jnp.concatenate([gate_weight, up_weight], 1)
    gate_share = lax.psum_scatter(
        jnp.dot(all_rows, w_both, preferred_element_type=jnp.float32).astype(jnp.bfloat16),
        "seq",
        scatter_dimension=0,
        tiled=True,
    ).astype(jnp.float32)
    hidden = swiglu(gate_share, half_cols)
    out_terms = jnp.dot(
        lax.all_gather(hidden, "seq", axis=0, tiled=True),
        down_weight,
        preferred_element_type=jnp.float32,
    )
    col_width = out_terms.shape[1]
    out_terms = out_terms.reshape(seq_count, tok_rows, col_width)
    summed = summed_on_arrival(out_terms.astype(jnp.bfloat16), "tp", 1)
    rounded = summed.astype(jnp.bfloat16)
    mixed_out = lax.all_to_all(rounded, "seq", split_axis=0, concat_axis=2, tiled=True)
    return mixed_out.reshape(mixed_out.shape[1], mixed_out.shape[2])


def solution(mesh):
    in_specs = (P("seq", None), P(), P(), P("seq", "tp"), P("seq", "tp"), P("tp", "seq"))
    out_specs = P(("seq", "tp"), None)
    return jax.shard_map(shards, mesh=mesh, in_specs=in_specs, out_specs=out_specs, check_vma=False)
```

profile of v0, /device:TPU:1, one launch (start us, length us, event | category | flops | bytes accessed | tf_op | source)
XLA Modules:
  0.0 350.1 jit_solution(9454202880680602987)
XLA Ops:
  6.5 0.0 copy-start
  6.5 0.0 reduce-scatter.2.cloned.1.call-start
  6.5 1.1 slice.34
  7.6 4.9 %collective-permute-start = (bf16[3,8192]{1,0:T(4,128)(2,1)S(1)}, bf16[3,8192]{1,0:T(4,128)(2,1)S(1)}, u32[]{:S(2)}, u32[]{:S(2)}) collective-permute-start(bf16[3,8192]{1,0:T(4,128)(2,1)S(1)} %slice.34), channel_id=1, source_target_pairs={{0,8},{8,16},{16,24},{24,32},{32,40},{40,48},{48,56},{56,64},{64,7... | collective-permute-start | bytes 147464 | tf_op jit(solution)/shard_map/ppermute | solution.py:10
  12.5 1.4 fusion.9
  13.9 4.1 %copy.16 = bf16[128,8192]{0,1:T(8,128)(2,1)} copy(bf16[128,8192]{1,0:T(8,128)(2,1)} %param.6) | data formatting | bytes 4194304 | tf_op args[0]
  18.0 0.0 collective-permute-done
  18.0 1.8 copy.15
  19.8 3.7 %maximum_convert_fusion = f32[131,8192]{0,1:T(8,128)S(1)} fusion(bf16[128,8192]{0,1:T(8,128)(2,1)} %copy.16, bf16[3,8192]{0,1:T(8,128)(2,1)} %copy.15), kind=kLoop, calls=%fused_computation.8 | loop fusion | flops 4292608 | bytes 6438912 | tf_op jit(solution)/shard_map/convert_element_type | solution.py:34
  23.6 0.0 copy-start.1
  23.6 8.7 %multiply_reduce_fusion = (f32[128]{0:T(128)S(1)}, f32[128,8192]{0,1:T(8,128)S(1)}) fusion(f32[131,8192]{0,1:T(8,128)S(1)} %maximum_convert_fusion, f32[8192]{0:T(1024)S(1)} %bitcast.30, f32[8192]{0:T(1024)S(1)} %bitcast.31, f32[8192]{0:T(1024)S(1)} %bitcast.29, f32[8192]{0:T(1024)S(1)} %bitcast.28), kind=kLoop, calls=%fused_computation.10 | loop fusion | flops 9437056 | bytes 21103104 | tf_op jit(solution)/shard_map/reduce_sum | solution.py:39
  32.3 0.0 copy-done.1
  32.3 3.5 multiply_convert_fusion
  35.8 35.4 %all_to_all.39 = bf16[128,16,512]{0,2,1:T(8,128)(2,1)} all-to-all(bf16[128,16,512]{0,2,1:T(8,128)(2,1)S(1)} %bitcast.22), channel_id=1, replica_groups=mesh['seq'=16,'tp'=8] {'seq'}, dimensions={1} | all-to-all | bytes 4194304 | tf_op jit(solution)/shard_map/all_to_all | solution.py:41
  71.2 3.9 %copy.17 = bf16[16,128,512]{2,1,0:T(8,128)(2,1)} copy(bf16[16,128,512]{1,2,0:T(8,128)(2,1)} %bitcast.23) | data formatting | bytes 4194304 | tf_op jit(solution)/shard_map/all_to_all | solution.py:41
  75.1 13.4 %convolution_convert_fusion = bf16[2048,3584]{1,0:T(8,128)(2,1)} fusion(bf16[2048,512]{1,0:T(8,128)(2,1)} %bitcast.25, bf16[512,1792]{1,0:T(8,128)(2,1)} %param.10, bf16[512,1792]{1,0:T(8,128)(2,1)} %param.9), kind=kOutput, calls=%fused_computation | convolution fusion | flops 7530872832 | bytes 20447232 | tf_op jit(solution)/shard_map/dot_general | solution.py:45
  88.5 0.0 reduce-scatter.2.cloned.1.call-update
  88.5 0.0 all-gather.2.cloned.1.call-start
  88.6 129.9 %reduce-scatter.2.cloned.1.call-done = bf16[128,3584]{1,0:T(8,128)(2,1)} async-done(((bf16[2048,3584]{1,0:T(8,128)(2,1)}), bf16[128,3584]{1,0:T(8,128)(2,1)}) %reduce-scatter.2.cloned.1.call-update) | async-done | bytes 917520 | tf_op jit(solution)/shard_map/reduce_scatter | solution.py:44
  218.4 1.4 convert_element_type.27
  219.8 1.0 fusion.6
  220.8 0.0 all-gather.2.cloned.1.call-update
  220.8 67.8 %all-gather.2.cloned.1.call-done = bf16[2048,1792]{1,0:T(8,128)(2,1)} async-done(((bf16[128,1792]{1,0:T(8,128)(2,1)}), bf16[2048,1792]{1,0:T(8,128)(2,1)}) %all-gather.2.cloned.1.call-update) | async-done | bytes 7340048 | tf_op jit(solution)/shard_map/all_gather | solution.py:52
  288.6 0.0 copy-done
  288.7 7.3 %convolution_convert_fusion.1 = bf16[2048,512]{1,0:T(8,128)(2,1)S(1)} fusion(bf16[2048,1792]{1,0:T(8,128)(2,1)} %all-gather.2.cloned.1.call-done, bf16[1792,512]{1,0:T(8,128)(2,1)S(1)} %copy-done), kind=kOutput, calls=%fused_computation.14 | convolution fusion | flops 3759144960 | bytes 11272192 | tf_op jit(solution)/shard_map/dot_general | solution.py:51
  295.9 0.2 copy.25
  296.1 30.1 %all_to_all.40 = bf16[8,16,16,512]{3,2,1,0:T(8,128)(2,1)} all-to-all(bf16[8,16,16,512]{3,2,1,0:T(8,128)(2,1)S(1)} %bitcast.24), channel_id=1, replica_groups=mesh['seq'=16,'tp'=8] {'tp'}, dimensions={0} | all-to-all | bytes 4194304 | tf_op jit(solution)/shard_map/all_to_all | solution.py:21
  326.2 2.0 reduce_sum.22
  328.2 14.4 %all_to_all.41 = bf16[16,16,512]{2,1,0:T(8,128)(2,1)S(1)} all-to-all(bf16[16,16,512]{2,1,0:T(8,128)(2,1)S(1)} %reduce_sum.22), channel_id=1, replica_groups=mesh['seq'=16,'tp'=8] {'seq'}, dimensions={0} | all-to-all | bytes 524288 | tf_op jit(solution)/shard_map/all_to_all | solution.py:60
  342.6 0.7 copy.22
  (1 shorter events, 0.0 us)
Async XLA Ops:
  6.5 282.1 %copy-start = (bf16[1792,512]{1,0:T(8,128)(2,1)S(1)}, bf16[1792,512]{1,0:T(8,128)(2,1)}, u32[]{:S(2)}) copy-start(bf16[1792,512]{1,0:T(8,128)(2,1)} %param.11) | copy-start | bytes 5505028
  6.5 211.9 %reduce-scatter.2.cloned.1.call-start = ((), (), s32[]{:S(2)}) async-start(), calls=%async_computation.4 | async-start | bytes 15597568 | tf_op jit(solution)/shard_map/reduce_scatter | solution.py:44
  7.6 10.4 %collective-permute-start = (bf16[3,8192]{1,0:T(4,128)(2,1)S(1)}, bf16[3,8192]{1,0:T(4,128)(2,1)S(1)}, u32[]{:S(2)}, u32[]{:S(2)}) collective-permute-start(bf16[3,8192]{1,0:T(4,128)(2,1)S(1)} %slice.34), channel_id=1, source_target_pairs={{0,8},{8,16},{16,24},{24,32},{32,40},{40,48},{48,56},{56,64},{64,7... | collective-permute-start | bytes 147464 | tf_op jit(solution)/shard_map/ppermute | solution.py:10
  23.6 8.8 %copy-start.1 = (f32[8192]{0:T(1024)S(1)}, f32[8192]{0:T(1024)}, u32[]{:S(2)}) copy-start(f32[8192]{0:T(1024)} %param.8) | copy-start | bytes 98308
  88.5 200.1 %all-gather.2.cloned.1.call-start = ((), (), s32[]{:S(2)}) async-start(), calls=%async_computation.5 | async-start | bytes 7798784 | tf_op jit(solution)/shard_map/all_gather | solution.py:52
Sparse Core Ops, SparseCore 0:
  88.6 129.7 reduce-scatter.1
  221.0 67.6 all-gather.1
where the time goes:
time: 351 us; the launch traced here: 350 us
  waiting for transfers between devices  198 us (56%)
  blocking collectives  79.8 us (23%)
  matrix products  20.6 us (6%)
  other arithmetic  20.3 us (6%)
  between operations  13.5 us (4%)
  local copies, waits for them, and re-layouts  13.2 us (4%)
  starting transfers between devices  4.97 us (1%)
    reduce_scatter x1, waiting for transfers between devices, shards(): lax.psum_scatter(jnp.dot(all_rows, w_both, preferred_element_type=jnp.flo...  130 us
    all_gather x1, waiting for transfers between devices, shards(): lax.all_gather(hidden, 'seq', axis=0, tiled=True)  67.8 us
    all_to_all x1, blocking collectives, shards(): lax.all_to_all(normed, 'seq', split_axis=1, concat_axis=0, tiled=True)  35.4 us
    all_to_all x1, blocking collectives, summed_on_arrival(): lax.all_to_all(parts, axis, split_axis=0, concat_axis=0, tiled=True)  30.1 us
    all_to_all x1, blocking collectives, shards(): lax.all_to_all(rounded, 'seq', split_axis=0, concat_axis=2, tiled=True)  14.4 us
    dot_general x1, matrix products, shards(): jnp.dot(all_rows, w_both, preferred_element_type=jnp.float32)  13.4 us
    reduce_sum x1, other arithmetic, shards(): jnp.mean(conv_out * conv_out, axis=-1, keepdims=True) + 1e-05  8.75 us
    dot_general x1, matrix products, shards(): jnp.dot(lax.all_gather(hidden, 'seq', axis=0, tiled=True), down_weight, p...  7.26 us
  transfers between devices with their start and end apart: 3, of which 2 were waited for; matrix products, arithmetic and copies ran while one was open for 2% of the time, Pallas kernels for 0%

commit v1 on v0

--- a/solution.py
+++ b/solution.py
@@ -2,6 +2,11 @@
 import jax.numpy as jnp
 from jax import lax
 from jax.sharding import PartitionSpec as P
+
+
+def exchange_gather(x, axis, along):
+    sent = jnp.stack([x] * lax.axis_size(axis))
+    return jnp.concatenate(lax.all_to_all(sent, axis, 0, 0), axis=along)
 
 
 def from_behind(shard, axis, by):
@@ -49,9 +54,7 @@
     ).astype(jnp.float32)
     hidden = swiglu(gate_share, half_cols)
     out_terms = jnp.dot(
-        lax.all_gather(hidden, "seq", axis=0, tiled=True),
-        down_weight,
-        preferred_element_type=jnp.float32,
+        exchange_gather(hidden, "seq", 0), down_weight, preferred_element_type=jnp.float32
     )
     col_width = out_terms.shape[1]
     out_terms = out_terms.reshape(seq_count, tok_rows, col_width)

time: 351 us -> 369 us (1.051)
  blocking collectives: 79.8 us -> 169 us
  waiting for transfers between devices: 198 us -> 130 us
    all_to_all x0 -> x1, blocking collectives: none -> 88.6 us  [exchange_gather(): return jnp.concatenate(lax.all_to_all(sent, axis, 0, 0), axis=along)]
    all_gather x1 -> x0, waiting for transfers between devices: 67.8 us -> none  [shards(): lax.all_gather(hidden, 'seq', axis=0, tiled=True)]
  transfers between devices with their start and end apart: 3 -> 2, of which waited for: 2 -> 1; matrix products, arithmetic and copies ran while one was open for 2% -> 1% of each run, Pallas kernels for 0% -> 0%
where the time goes in v1:
time: 369 us
  blocking collectives  169 us (46%)
  waiting for transfers between devices  130 us (35%)
  other arithmetic  19.5 us (5%)
  matrix products  17.5 us (5%)
  local copies, waits for them, and re-layouts  13.9 us (4%)
  between operations  13.5 us (4%)
  starting transfers between devices  4.93 us (1%)
    reduce_scatter x1, waiting for transfers between devices, shards(): lax.psum_scatter(jnp.dot(all_rows, w_both, preferred_element_type=jnp.flo...  130 us
    all_to_all x1, blocking collectives, exchange_gather(): return jnp.concatenate(lax.all_to_all(sent, axis, 0, 0), axis=along)  88.6 us
    all_to_all x1, blocking collectives, shards(): lax.all_to_all(normed, 'seq', split_axis=1, concat_axis=0, tiled=True)  35.4 us
    all_to_all x1, blocking collectives, summed_on_arrival(): lax.all_to_all(parts, axis, split_axis=0, concat_axis=0, tiled=True)  30.3 us
    all_to_all x1, blocking collectives, shards(): lax.all_to_all(rounded, 'seq', split_axis=0, concat_axis=2, tiled=True)  15.1 us
    dot_general x1, matrix products, shards(): jnp.dot(all_rows, w_both, preferred_element_type=jnp.float32)  13.4 us
    reduce_sum x1, other arithmetic, shards(): jnp.mean(conv_out * conv_out, axis=-1, keepdims=True) + 1e-05  8.75 us
  transfers between devices with their start and end apart: 2, of which 1 were waited for; matrix products, arithmetic and copies ran while one was open for 1% of the time, Pallas kernels for 0%

profile of v1, /device:TPU:1, one launch (start us, length us, event | category | flops | bytes accessed | tf_op | source)
XLA Modules:
  0.0 368.5 jit_solution(6847087268541967688)
XLA Ops:
  6.5 0.0 copy-start
  6.5 0.0 reduce-scatter.2.cloned.1.call-start
  6.5 1.1 slice.34
  7.6 4.9 %collective-permute-start = (bf16[3,8192]{1,0:T(4,128)(2,1)S(1)}, bf16[3,8192]{1,0:T(4,128)(2,1)S(1)}, u32[]{:S(2)}, u32[]{:S(2)}) collective-permute-start(bf16[3,8192]{1,0:T(4,128)(2,1)S(1)} %slice.34), channel_id=1, source_target_pairs={{0,8},{8,16},{16,24},{24,32},{32,40},{40,48},{48,56},{56,64},{64,7... | collective-permute-start | bytes 147464 | tf_op jit(solution)/shard_map/ppermute | solution.py:15
  12.5 1.4 fusion.10
  13.9 4.1 %copy.16 = bf16[128,8192]{0,1:T(8,128)(2,1)} copy(bf16[128,8192]{1,0:T(8,128)(2,1)} %param.6) | data formatting | bytes 4194304 | tf_op args[0]
  18.0 0.0 collective-permute-done
  18.0 1.8 copy.15
  19.9 3.7 %maximum_convert_fusion = f32[131,8192]{0,1:T(8,128)S(1)} fusion(bf16[128,8192]{0,1:T(8,128)(2,1)} %copy.16, bf16[3,8192]{0,1:T(8,128)(2,1)} %copy.15), kind=kLoop, calls=%fused_computation.8 | loop fusion | flops 4292608 | bytes 6438912 | tf_op jit(solution)/shard_map/convert_element_type | solution.py:39
  23.6 0.0 copy-start.1
  23.6 8.7 %multiply_reduce_fusion = (f32[128]{0:T(128)S(1)}, f32[128,8192]{0,1:T(8,128)S(1)}) fusion(f32[131,8192]{0,1:T(8,128)S(1)} %maximum_convert_fusion, f32[8192]{0:T(1024)S(1)} %bitcast.32, f32[8192]{0:T(1024)S(1)} %bitcast.33, f32[8192]{0:T(1024)S(1)} %bitcast.31, f32[8192]{0:T(1024)S(1)} %bitcast.30), kind=kLoop, calls=%fused_computation.10 | loop fusion | flops 9437056 | bytes 21103104 | tf_op jit(solution)/shard_map/reduce_sum | solution.py:44
  32.4 0.0 copy-done.1
  32.4 3.5 multiply_convert_fusion
  35.9 35.4 %all_to_all.44 = bf16[128,16,512]{0,2,1:T(8,128)(2,1)} all-to-all(bf16[128,16,512]{0,2,1:T(8,128)(2,1)S(1)} %bitcast.24), channel_id=1, replica_groups=mesh['seq'=16,'tp'=8] {'seq'}, dimensions={1} | all-to-all | bytes 4194304 | tf_op jit(solution)/shard_map/all_to_all | solution.py:46
  71.2 3.9 %copy.17 = bf16[16,128,512]{2,1,0:T(8,128)(2,1)} copy(bf16[16,128,512]{1,2,0:T(8,128)(2,1)} %bitcast.25) | data formatting | bytes 4194304 | tf_op jit(solution)/shard_map/all_to_all | solution.py:46
  75.1 13.4 %convolution_convert_fusion = bf16[2048,3584]{1,0:T(8,128)(2,1)} fusion(bf16[2048,512]{1,0:T(8,128)(2,1)} %bitcast.27, bf16[512,1792]{1,0:T(8,128)(2,1)} %param.10, bf16[512,1792]{1,0:T(8,128)(2,1)} %param.9), kind=kOutput, calls=%fused_computation | convolution fusion | flops 7530872832 | bytes 20447232 | tf_op jit(solution)/shard_map/dot_general | solution.py:50
  88.5 0.0 reduce-scatter.2.cloned.1.call-update
  88.5 129.9 %reduce-scatter.2.cloned.1.call-done = bf16[128,3584]{1,0:T(8,128)(2,1)} async-done(((bf16[2048,3584]{1,0:T(8,128)(2,1)}), bf16[128,3584]{1,0:T(8,128)(2,1)}) %reduce-scatter.2.cloned.1.call-update) | async-done | bytes 917520 | tf_op jit(solution)/shard_map/reduce_scatter | solution.py:49
  218.4 1.4 convert_element_type.23
  219.7 0.3 fusion.7
  220.0 0.7 stack.2
  220.7 88.6 %all_to_all.45 = bf16[16,128,1792]{2,1,0:T(8,128)(2,1)S(1)} all-to-all(bf16[16,128,1792]{2,1,0:T(8,128)(2,1)S(1)} %stack.2), channel_id=1, replica_groups=mesh['seq'=16,'tp'=8] {'seq'}, dimensions={0} | all-to-all | bytes 14680064 | tf_op jit(solution)/shard_map/all_to_all | solution.py:9
  309.3 0.0 copy-done
  309.3 4.1 %convolution_convert_fusion.1 = bf16[16,128,512]{2,1,0:T(8,128)(2,1)S(1)} fusion(bf16[16,128,1792]{2,1,0:T(8,128)(2,1)S(1)} %all_to_all.45, bf16[1792,512]{1,0:T(8,128)(2,1)S(1)} %copy-done), kind=kOutput, calls=%fused_computation.15 | convolution fusion | flops 3759144960 | bytes 11272192 | tf_op jit(solution)/shard_map/dot_general | solution.py:56
  313.4 0.2 copy.25
  313.6 30.3 %all_to_all.46 = bf16[8,16,16,512]{3,2,1,0:T(8,128)(2,1)} all-to-all(bf16[8,16,16,512]{3,2,1,0:T(8,128)(2,1)S(1)} %bitcast.26), channel_id=1, replica_groups=mesh['seq'=16,'tp'=8] {'tp'}, dimensions={0} | all-to-all | bytes 4194304 | tf_op jit(solution)/shard_map/all_to_all | solution.py:26
  343.9 2.0 reduce_sum.22
  345.9 15.1 %all_to_all.47 = bf16[16,16,512]{2,1,0:T(8,128)(2,1)S(1)} all-to-all(bf16[16,16,512]{2,1,0:T(8,128)(2,1)S(1)} %reduce_sum.22), channel_id=1, replica_groups=mesh['seq'=16,'tp'=8] {'seq'}, dimensions={0} | all-to-all | bytes 524288 | tf_op jit(solution)/shard_map/all_to_all | solution.py:63
  360.9 0.7 copy.22
  (1 shorter events, 0.0 us)
Async XLA Ops:
  6.5 302.8 %copy-start = (bf16[1792,512]{1,0:T(8,128)(2,1)S(1)}, bf16[1792,512]{1,0:T(8,128)(2,1)}, u32[]{:S(2)}) copy-start(bf16[1792,512]{1,0:T(8,128)(2,1)} %param.11) | copy-start | bytes 5505028
  6.5 211.8 %reduce-scatter.2.cloned.1.call-start = ((), (), s32[]{:S(2)}) async-start(), calls=%async_computation.5 | async-start | bytes 15597568 | tf_op jit(solution)/shard_map/reduce_scatter | solution.py:49
  7.6 10.4 %collective-permute-start = (bf16[3,8192]{1,0:T(4,128)(2,1)S(1)}, bf16[3,8192]{1,0:T(4,128)(2,1)S(1)}, u32[]{:S(2)}, u32[]{:S(2)}) collective-permute-start(bf16[3,8192]{1,0:T(4,128)(2,1)S(1)} %slice.34), channel_id=1, source_target_pairs={{0,8},{8,16},{16,24},{24,32},{32,40},{40,48},{48,56},{56,64},{64,7... | collective-permute-start | bytes 147464 | tf_op jit(solution)/shard_map/ppermute | solution.py:15
  23.6 8.8 %copy-start.1 = (f32[8192]{0:T(1024)S(1)}, f32[8192]{0:T(1024)}, u32[]{:S(2)}) copy-start(f32[8192]{0:T(1024)} %param.8) | copy-start | bytes 98308
Sparse Core Ops, SparseCore 0:
  88.6 129.6 reduce-scatter.1
